TPU v7x, 32 devices: a whole 2x2x4 slice. The times are simulated.
32 devices in a mesh: rows: 4 (over y, core), cols: 4 (over z), heads: 2 (over x).
Axes of the slice: x: 2, y: 2, z: 4, core: 2. Of those that a mesh axis runs over, the one named last changes fastest.
Arguments:
- tokens: bfloat16 [16384, 1024], P(('rows', 'cols'), 'heads'), may hold values from -8 to 8
- ln_gain: float32 [1024], replicated, may hold values from 0.1 to 1.9
- w_qkv: bfloat16 [3, 1024, 1024], P(None, None, 'heads'), may hold values from -1 to 1
- w_out: bfloat16 [1024, 1024], P('heads'), may hold values from -0.1875 to 0.1875
- out_bias: float32 [1024], P('heads'), may hold values from -3 to 3
Outputs:
- mixed: bfloat16 [16384, 1024], P(('rows', 'cols'), 'heads')
All inputs are finite; a program needn't handle non-finite values.
Results may differ from a plain program's by a relative error of at most 0.0095.
Values may be sent and summed in bfloat16 or wider, within the bound.
A program may use at most 128 MiB of HBM per device.

v0:
```python
import jax
import jax.numpy as jnp
from jax import lax
from jax.sharding import PartitionSpec as P

D = 1024
HEADS = 16


def attend_keys(carry, keys, values, queries, scale):

    def one_block(args):
        rows, peak, total, accum = args
        scores = jnp.einsum("qhe,khe->hqk", rows, keys, preferred_element_type=jnp.float32) * scale
        newpeak = jnp.maximum(peak, jnp.max(scores, axis=-1))
        weights = jnp.exp(scores - newpeak[..., None])
        factor = jnp.exp(peak - newpeak)
        total = total * factor + jnp.sum(weights, axis=-1)
        accum = accum * factor[..., None] + jnp.einsum(
            "hqk,khe->hqe", weights.astype(jnp.bfloat16), values, preferred_element_type=jnp.float32
        )
        return (newpeak, total, accum)

    peak, total, accum = carry
    return lax.map(one_block, (queries, peak, total, accum))


def per_device(tokens, ln_gain, w_qkv, w_out, out_bias):
    whole = lax.all_gather(tokens, "heads", axis=1, tiled=True)
    xf = whole.astype(jnp.float32)
    mean = jnp.mean(xf, axis=-1, keepdims=True)
    centered = xf - mean
    var = jnp.mean(centered * centered, axis=-1, keepdims=True)
    normed = (centered * lax.rsqrt(var + 1e-06) * ln_gain).astype(jnp.bfloat16)
    projected = jnp.einsum("td,sde->ste", normed, w_qkv, preferred_element_type=jnp.float32).astype(
        jnp.bfloat16
    )
    head_dim = D // HEADS
    local_heads = w_out.shape[0] // head_dim
    tok_rows = tokens.shape[0]
    qblock = 512
    qcount = tok_rows // qblock
    scale = 1.0 / head_dim**0.5
    queries = projected[0].reshape(qcount, qblock, local_heads, head_dim)
    keys_local = projected[1]
    values_local = projected[2]
    initial = (
        jnp.full((qcount, local_heads, qblock), -jnp.inf, jnp.float32),
        jnp.zeros((qcount, local_heads, qblock), jnp.float32),
        jnp.zeros((qcount, local_heads, qblock, head_dim), jnp.float32),
    )
    keys = lax.all_gather(keys_local, ("rows", "cols"), axis=0, tiled=True)
    values = lax.all_gather(values_local, ("rows", "cols"), axis=0, tiled=True)
    count = keys.shape[0]
    kblock = 1024
    kblocks = keys.reshape(count // kblock, kblock, local_heads, head_dim)
    vblocks = values.reshape(count // kblock, kblock, local_heads, head_dim)

    def step(state, pair):
        return (attend_keys(state, pair[0], pair[1], queries, scale), None)

    result, unused = lax.scan(step, initial, (kblocks, vblocks))
    peak, total, accum = result
    attended = accum / total[..., None]
    attended = (
        attended.transpose(0, 2, 1, 3)
        .reshape(tok_rows, local_heads * head_dim)
        .astype(jnp.bfloat16)
    )
    partial_value = jnp.dot(attended, w_out, preferred_element_type=jnp.float32)
    summed = lax.psum_scatter(
        partial_value.astype(jnp.bfloat16), "heads", scatter_dimension=1, tiled=True
    ).astype(jnp.float32)
    return (tokens.astype(jnp.float32) + summed + out_bias).astype(jnp.bfloat16)


def solution(mesh):
    return jax.shard_map(
        per_device,
        mesh=mesh,
        in_specs=(
            P(("rows", "cols"), "heads"),
            P(),
            P(None, None, "heads"),
            P("heads", None),
            P("heads"),
        ),
        out_specs=P(("rows", "cols"), "heads"),
        check_vma=False,
    )
```

profile of v0, /device:TPU:0, one launch (start us, length us, event | category | flops | bytes accessed | tf_op | source)
XLA Modules:
  0.0 804.4 jit_solution(14423901690388378114)
XLA Ops:
  7.3 37.4 %all-gather.6.cloned.1.call-done = bf16[1024,1024]{1,0:T(8,128)(2,1)} async-done(((bf16[1024,512]{1,0:T(8,128)(2,1)}), bf16[1024,1024]{1,0:T(8,128)(2,1)}) %all-gather.6.cloned.1.call-update) | async-done | bytes 2097168 | tf_op jit(solution)/shard_map/all_gather | solution.py:29
  58.2 123.1 %all-gather.8.cloned.1.call-done = bf16[1,16384,512]{2,1,0:T(8,128)(2,1)} async-done(((bf16[1,1024,512]{2,1,0:T(8,128)(2,1)}), bf16[1,16384,512]{2,1,0:T(8,128)(2,1)}) %all-gather.8.cloned.1.call-update) | async-done | bytes 16777232 | tf_op jit(solution)/shard_map/all_gather | solution.py:52
  181.3 41.4 %reshape.50 = bf16[16,1024,8,64]{3,2,1,0:T(8,128)(2,1)} reshape(bf16[1,16384,512]{2,1,0:T(8,128)(2,1)} %all-gather.8.cloned.1.call-done) | data formatting | bytes 33554432 | tf_op jit(solution)/shard_map/reshape | solution.py:56
  222.7 35.9 %copy.12 = bf16[16,1024,8,64]{1,3,2,0:T(8,128)(2,1)} copy(bf16[16,1024,8,64]{3,2,1,0:T(8,128)(2,1)} %reshape.50) | data formatting | bytes 33554432 | tf_op jit(solution)/shard_map/while | solution.py:62
  258.6 49.6 %all-gather.10.cloned.1.call-done = bf16[1,16384,512]{2,1,0:T(8,128)(2,1)} async-done(((bf16[1,1024,512]{2,1,0:T(8,128)(2,1)}), bf16[1,16384,512]{2,1,0:T(8,128)(2,1)}) %all-gather.10.cloned.1.call-update) | async-done | bytes 16777232 | tf_op jit(solution)/shard_map/all_gather | solution.py:53
  308.1 41.3 %reshape.51 = bf16[16,1024,8,64]{3,2,1,0:T(8,128)(2,1)} reshape(bf16[1,16384,512]{2,1,0:T(8,128)(2,1)} %all-gather.10.cloned.1.call-done) | data formatting | bytes 33554432 | tf_op jit(solution)/shard_map/reshape | solution.py:57
  349.5 35.4 %copy.13 = bf16[16,1024,8,64]{1,3,2,0:T(8,128)(2,1)} copy(bf16[16,1024,8,64]{3,2,1,0:T(8,128)(2,1)} %reshape.51) | data formatting | bytes 33554432 | tf_op jit(solution)/shard_map/while | solution.py:62
  386.5 372.3 %while.30 = (s32[]{:T(128)}, f32[2,8,512]{2,1,0:T(8,128)S(1)}, f32[2,8,512]{2,1,0:T(8,128)S(1)}, f32[2,8,512,64]{2,3,1,0:T(8,128)}, bf16[16,1024,8,64]{1,3,2,0:T...) while((s32[]{:T(128)}, f32[2,8,512]{2,1,0:T(8,128)S(1)}, ...), condition=%wide.region_7.8_spmd, body=%wide.region_2.7_spmd.sunk | while | flops 1107836928 | bytes 86753680 | solution.py:62
  388.3 21.5 %while.31 = (s32[]{:T(128)}, f32[2,8,512]{2,1,0:T(8,128)S(1)}, f32[2,8,512]{2,1,0:T(8,128)S(1)}, f32[2,8,512,64]{2,3,1,0:T(8,128)}, bf16[2,512,8,64]{1,3,2,0:T(8...) while((s32[]{:T(128)}, f32[2,8,512]{2,1,0:T(8,128)S(1)}, ...), condition=%wide.region_6.6_spmd.clone, body=%wide.region_3.5_spmd.clone.sunk | while | flops 1107836928 | bytes 82559200 | solution.py:25
  390.9 4.5 fusion.51
  401.7 4.5 fusion.51
  411.5 21.5 %while.31 = (s32[]{:T(128)}, f32[2,8,512]{2,1,0:T(8,128)S(1)}, f32[2,8,512]{2,1,0:T(8,128)S(1)}, f32[2,8,512,64]{2,3,1,0:T(8,128)}, bf16[2,512,8,64]{1,3,2,0:T(8...) while((s32[]{:T(128)}, f32[2,8,512]{2,1,0:T(8,128)S(1)}, ...), condition=%wide.region_6.6_spmd.clone, body=%wide.region_3.5_spmd.clone.sunk | while | flops 1107836928 | bytes 82559200 | solution.py:25
  414.2 4.5 fusion.51
  424.9 4.5 fusion.51
  434.8 21.5 %while.31 = (s32[]{:T(128)}, f32[2,8,512]{2,1,0:T(8,128)S(1)}, f32[2,8,512]{2,1,0:T(8,128)S(1)}, f32[2,8,512,64]{2,3,1,0:T(8,128)}, bf16[2,512,8,64]{1,3,2,0:T(8...) while((s32[]{:T(128)}, f32[2,8,512]{2,1,0:T(8,128)S(1)}, ...), condition=%wide.region_6.6_spmd.clone, body=%wide.region_3.5_spmd.clone.sunk | while | flops 1107836928 | bytes 82559200 | solution.py:25
  437.5 4.5 fusion.51
  448.2 4.5 fusion.51
  458.1 21.5 %while.31 = (s32[]{:T(128)}, f32[2,8,512]{2,1,0:T(8,128)S(1)}, f32[2,8,512]{2,1,0:T(8,128)S(1)}, f32[2,8,512,64]{2,3,1,0:T(8,128)}, bf16[2,512,8,64]{1,3,2,0:T(8...) while((s32[]{:T(128)}, f32[2,8,512]{2,1,0:T(8,128)S(1)}, ...), condition=%wide.region_6.6_spmd.clone, body=%wide.region_3.5_spmd.clone.sunk | while | flops 1107836928 | bytes 82559200 | solution.py:25
  460.7 4.5 fusion.51
  471.5 4.5 fusion.51
  481.3 21.5 %while.31 = (s32[]{:T(128)}, f32[2,8,512]{2,1,0:T(8,128)S(1)}, f32[2,8,512]{2,1,0:T(8,128)S(1)}, f32[2,8,512,64]{2,3,1,0:T(8,128)}, bf16[2,512,8,64]{1,3,2,0:T(8...) while((s32[]{:T(128)}, f32[2,8,512]{2,1,0:T(8,128)S(1)}, ...), condition=%wide.region_6.6_spmd.clone, body=%wide.region_3.5_spmd.clone.sunk | while | flops 1107836928 | bytes 82559200 | solution.py:25
  484.0 4.5 fusion.51
  504.6 21.5 %while.31 = (s32[]{:T(128)}, f32[2,8,512]{2,1,0:T(8,128)S(1)}, f32[2,8,512]{2,1,0:T(8,128)S(1)}, f32[2,8,512,64]{2,3,1,0:T(8,128)}, bf16[2,512,8,64]{1,3,2,0:T(8...) while((s32[]{:T(128)}, f32[2,8,512]{2,1,0:T(8,128)S(1)}, ...), condition=%wide.region_6.6_spmd.clone, body=%wide.region_3.5_spmd.clone.sunk | while | flops 1107836928 | bytes 82559200 | solution.py:25
  507.3 4.5 fusion.51
  527.9 21.5 %while.31 = (s32[]{:T(128)}, f32[2,8,512]{2,1,0:T(8,128)S(1)}, f32[2,8,512]{2,1,0:T(8,128)S(1)}, f32[2,8,512,64]{2,3,1,0:T(8,128)}, bf16[2,512,8,64]{1,3,2,0:T(8...) while((s32[]{:T(128)}, f32[2,8,512]{2,1,0:T(8,128)S(1)}, ...), condition=%wide.region_6.6_spmd.clone, body=%wide.region_3.5_spmd.clone.sunk | while | flops 1107836928 | bytes 82559200 | solution.py:25
  541.3 4.5 fusion.51
  551.2 21.5 %while.31 = (s32[]{:T(128)}, f32[2,8,512]{2,1,0:T(8,128)S(1)}, f32[2,8,512]{2,1,0:T(8,128)S(1)}, f32[2,8,512,64]{2,3,1,0:T(8,128)}, bf16[2,512,8,64]{1,3,2,0:T(8...) while((s32[]{:T(128)}, f32[2,8,512]{2,1,0:T(8,128)S(1)}, ...), condition=%wide.region_6.6_spmd.clone, body=%wide.region_3.5_spmd.clone.sunk | while | flops 1107836928 | bytes 82559200 | solution.py:25
  564.5 4.5 fusion.51
  574.4 21.5 %while.31 = (s32[]{:T(128)}, f32[2,8,512]{2,1,0:T(8,128)S(1)}, f32[2,8,512]{2,1,0:T(8,128)S(1)}, f32[2,8,512,64]{2,3,1,0:T(8,128)}, bf16[2,512,8,64]{1,3,2,0:T(8...) while((s32[]{:T(128)}, f32[2,8,512]{2,1,0:T(8,128)S(1)}, ...), condition=%wide.region_6.6_spmd.clone, body=%wide.region_3.5_spmd.clone.sunk | while | flops 1107836928 | bytes 82559200 | solution.py:25
  587.8 4.5 fusion.51
  597.7 21.5 %while.31 = (s32[]{:T(128)}, f32[2,8,512]{2,1,0:T(8,128)S(1)}, f32[2,8,512]{2,1,0:T(8,128)S(1)}, f32[2,8,512,64]{2,3,1,0:T(8,128)}, bf16[2,512,8,64]{1,3,2,0:T(8...) while((s32[]{:T(128)}, f32[2,8,512]{2,1,0:T(8,128)S(1)}, ...), condition=%wide.region_6.6_spmd.clone, body=%wide.region_3.5_spmd.clone.sunk | while | flops 1107836928 | bytes 82559200 | solution.py:25
  600.4 4.5 fusion.51
  611.1 4.5 fusion.51
  621.0 21.5 %while.31 = (s32[]{:T(128)}, f32[2,8,512]{2,1,0:T(8,128)S(1)}, f32[2,8,512]{2,1,0:T(8,128)S(1)}, f32[2,8,512,64]{2,3,1,0:T(8,128)}, bf16[2,512,8,64]{1,3,2,0:T(8...) while((s32[]{:T(128)}, f32[2,8,512]{2,1,0:T(8,128)S(1)}, ...), condition=%wide.region_6.6_spmd.clone, body=%wide.region_3.5_spmd.clone.sunk | while | flops 1107836928 | bytes 82559200 | solution.py:25
  623.6 4.5 fusion.51
  644.2 21.5 %while.31 = (s32[]{:T(128)}, f32[2,8,512]{2,1,0:T(8,128)S(1)}, f32[2,8,512]{2,1,0:T(8,128)S(1)}, f32[2,8,512,64]{2,3,1,0:T(8,128)}, bf16[2,512,8,64]{1,3,2,0:T(8...) while((s32[]{:T(128)}, f32[2,8,512]{2,1,0:T(8,128)S(1)}, ...), condition=%wide.region_6.6_spmd.clone, body=%wide.region_3.5_spmd.clone.sunk | while | flops 1107836928 | bytes 82559200 | solution.py:25
  646.9 4.5 fusion.51
  657.6 4.5 fusion.51
  667.5 21.5 %while.31 = (s32[]{:T(128)}, f32[2,8,512]{2,1,0:T(8,128)S(1)}, f32[2,8,512]{2,1,0:T(8,128)S(1)}, f32[2,8,512,64]{2,3,1,0:T(8,128)}, bf16[2,512,8,64]{1,3,2,0:T(8...) while((s32[]{:T(128)}, f32[2,8,512]{2,1,0:T(8,128)S(1)}, ...), condition=%wide.region_6.6_spmd.clone, body=%wide.region_3.5_spmd.clone.sunk | while | flops 1107836928 | bytes 82559200 | solution.py:25
  670.2 4.5 fusion.51
  690.8 21.5 %while.31 = (s32[]{:T(128)}, f32[2,8,512]{2,1,0:T(8,128)S(1)}, f32[2,8,512]{2,1,0:T(8,128)S(1)}, f32[2,8,512,64]{2,3,1,0:T(8,128)}, bf16[2,512,8,64]{1,3,2,0:T(8...) while((s32[]{:T(128)}, f32[2,8,512]{2,1,0:T(8,128)S(1)}, ...), condition=%wide.region_6.6_spmd.clone, body=%wide.region_3.5_spmd.clone.sunk | while | flops 1107836928 | bytes 82559200 | solution.py:25
  693.4 4.5 fusion.51
  704.2 4.5 fusion.51
  714.0 21.5 %while.31 = (s32[]{:T(128)}, f32[2,8,512]{2,1,0:T(8,128)S(1)}, f32[2,8,512]{2,1,0:T(8,128)S(1)}, f32[2,8,512,64]{2,3,1,0:T(8,128)}, bf16[2,512,8,64]{1,3,2,0:T(8...) while((s32[]{:T(128)}, f32[2,8,512]{2,1,0:T(8,128)S(1)}, ...), condition=%wide.region_6.6_spmd.clone, body=%wide.region_3.5_spmd.clone.sunk | while | flops 1107836928 | bytes 82559200 | solution.py:25
  716.7 4.5 fusion.51
  737.3 21.5 %while.31 = (s32[]{:T(128)}, f32[2,8,512]{2,1,0:T(8,128)S(1)}, f32[2,8,512]{2,1,0:T(8,128)S(1)}, f32[2,8,512,64]{2,3,1,0:T(8,128)}, bf16[2,512,8,64]{1,3,2,0:T(8...) while((s32[]{:T(128)}, f32[2,8,512]{2,1,0:T(8,128)S(1)}, ...), condition=%wide.region_6.6_spmd.clone, body=%wide.region_3.5_spmd.clone.sunk | while | flops 1107836928 | bytes 82559200 | solution.py:25
  740.0 4.5 fusion.51
  764.8 30.2 %reduce-scatter.2.cloned.1.call-done = bf16[1024,512]{1,0:T(8,128)(2,1)} async-done(((bf16[1024,1024]{1,0:T(8,128)(2,1)}), bf16[1024,512]{1,0:T(8,128)(2,1)}) %reduce-scatter.2.cloned.1.call-update) | async-done | bytes 1048592 | tf_op jit(solution)/shard_map/reduce_scatter | solution.py:71
  (477 shorter events, 288.5 us)
Async XLA Ops:
  6.5 42.6 %copy-start = (bf16[3,1024,512]{2,1,0:T(8,128)(2,1)S(1)}, bf16[3,1024,512]{2,1,0:T(8,128)(2,1)}, u32[]{:S(2)}) copy-start(bf16[3,1024,512]{2,1,0:T(8,128)(2,1)} %param.11) | copy-start | bytes 9437188
  6.5 42.6 %copy-start.9 = (f32[1024]{0:T(1024)S(1)}, f32[1024]{0:T(1024)}, u32[]{:S(2)}) copy-start(f32[1024]{0:T(1024)} %param.10) | copy-start | bytes 12292
  6.5 38.2 %all-gather.6.cloned.1.call-start = ((), (), s32[]{:S(2)}) async-start(), calls=%async_computation.1 | async-start | bytes 3145728 | tf_op jit(solution)/shard_map/all_gather | solution.py:29
  7.3 174.0 %all-gather.8.cloned.1.call-start = ((), (), s32[]{:S(2)}) async-start(), calls=%async_computation.3 | async-start | bytes 17825792 | tf_op jit(solution)/shard_map/all_gather | solution.py:52
  44.7 4.4 copy-start.6
  54.7 253.4 %all-gather.10.cloned.1.call-start = ((), (), s32[]{:S(2)}) async-start(), calls=%async_computation.4 | async-start | bytes 17825792 | tf_op jit(solution)/shard_map/all_gather | solution.py:53
  55.5 739.6 %reduce-scatter.2.cloned.1.call-start = ((), (), s32[]{:S(2)}) async-start(), calls=%async_computation.2 | async-start | bytes 3145728 | tf_op jit(solution)/shard_map/reduce_scatter | solution.py:71
  395.5 3.5 copy-start.3
  395.5 3.5 copy-start.5
  406.2 3.5 copy-start.3
  406.2 3.5 copy-start.5
  418.7 3.5 copy-start.3
  418.7 3.5 copy-start.5
  429.5 3.5 copy-start.3
  429.5 3.5 copy-start.5
  442.0 3.5 copy-start.3
  442.0 3.5 copy-start.5
  452.7 3.5 copy-start.3
  452.7 3.5 copy-start.5
  465.3 3.5 copy-start.3
  465.3 3.5 copy-start.5
  476.0 3.5 copy-start.5
  488.5 3.5 copy-start.5
  499.3 3.5 copy-start.5
  511.8 3.5 copy-start.5
  522.5 3.5 copy-start.5
  535.1 3.5 copy-start.5
  545.8 3.5 copy-start.5
  558.4 3.5 copy-start.5
  569.1 3.5 copy-start.5
  581.6 3.5 copy-start.5
  592.4 3.5 copy-start.5
  604.9 3.5 copy-start.5
  615.7 3.5 copy-start.5
  628.2 3.5 copy-start.5
  638.9 3.5 copy-start.5
  651.5 3.5 copy-start.5
  662.2 3.5 copy-start.5
  674.7 3.5 copy-start.5
  685.5 3.5 copy-start.5
  698.0 3.5 copy-start.5
  708.7 3.5 copy-start.5
  721.3 3.5 copy-start.5
  732.0 3.5 copy-start.5
  744.5 3.5 copy-start.5
  755.3 3.5 copy-start.5
  762.1 32.9 %copy-start.7 = (f32[512]{0:T(512)S(1)}, f32[512]{0:T(512)}, u32[]{:S(2)}) copy-start(f32[512]{0:T(512)} %param.13) | copy-start | bytes 6148
  762.1 35.7 %copy-start.1 = (bf16[3,1024,512]{2,1,0:T(8,128)(2,1)S(1)}, bf16[3,1024,512]{2,1,0:T(8,128)(2,1)}, u32[]{:S(2)}) copy-start(bf16[3,1024,512]{2,1,0:T(8,128)(2,1)} %param.11) | copy-start | bytes 9437188
  (90 other events, 250.4 us)
Sparse Core Ops, SparseCore 0:
  8.9 35.8 all-gather.5
  54.8 126.4 all-gather.7
  183.5 124.5 all-gather.9
  764.9 30.0 reduce-scatter.1
where the time goes:
time: 809 us; the launch traced here: 804 us
  waiting for transfers between devices  242 us (30%)
  matrix products  231 us (29%)
  local copies, waits for them, and re-layouts  194 us (24%)
  other arithmetic  121 us (15%)
  between operations  13.3 us (2%)
    dot_general x32, matrix products, one_block(): jnp.einsum('hqk,khe->hqe', weights.astype(jnp.bfloat16), values, preferre...  145 us
    all_gather x1, waiting for transfers between devices, per_device(): keys = lax.all_gather(keys_local, ('rows', 'cols'), axis=0, tiled=True)  123 us
    reduce_sum x32, other arithmetic, one_block(): total = total * factor + jnp.sum(weights, axis=-1)  110 us
    dot_general x32, matrix products, one_block(): jnp.einsum('qhe,khe->hqk', rows, keys, preferred_element_type=jnp.float32)  78.9 us
    while x3, local copies, waits for them, and re-layouts, per_device(): result, unused = lax.scan(step, initial, (kblocks, vblocks))  72.7 us
    all_gather x1, waiting for transfers between devices, per_device(): values = lax.all_gather(values_local, ('rows', 'cols'), axis=0, tiled=True)  49.6 us
    reshape x1, local copies, waits for them, and re-layouts, per_device(): kblocks = keys.reshape(count // kblock, kblock, local_heads, head_dim)  41.4 us
    reshape x1, local copies, waits for them, and re-layouts, per_device(): vblocks = values.reshape(count // kblock, kblock, local_heads, head_dim)  41.3 us
  transfers between devices with their start and end apart: 4, of which 4 were waited for; matrix products, arithmetic and copies ran while one was open for 10% of the time, Pallas kernels for 0%

commit v1 on v0

--- a/solution.py
+++ b/solution.py
@@ -49,8 +49,16 @@
         jnp.zeros((qcount, local_heads, qblock), jnp.float32),
         jnp.zeros((qcount, local_heads, qblock, head_dim), jnp.float32),
     )
-    keys = lax.all_gather(keys_local, ("rows", "cols"), axis=0, tiled=True)
-    values = lax.all_gather(values_local, ("rows", "cols"), axis=0, tiled=True)
+    keys, values = jnp.split(
+        lax.all_gather(
+            jnp.concatenate([keys_local, values_local], axis=1),
+            ("rows", "cols"),
+            axis=0,
+            tiled=True,
+        ),
+        [keys_local.shape[1]],
+        axis=1,
+    )
     count = keys.shape[0]
     kblock = 1024
     kblocks = keys.reshape(count // kblock, kblock, local_heads, head_dim)

time: 809 us -> 739 us (0.913)
  local copies, waits for them, and re-layouts: 194 us -> 121 us
    reshape x2 -> x0, local copies, waits for them, and re-layouts: 82.7 us -> none  [the longest x1 41.4 us: per_device(): kblocks = keys.reshape(count // kblock, kblock, local_heads, head_dim)]
    while x3, local copies, waits for them, and re-layouts: 72.7 us -> 41.4 us  [per_device(): result, unused = lax.scan(step, initial, (kblocks, vblocks))]
    unnamed x13 -> x15, local copies, waits for them, and re-layouts: 0.27 us -> 26.3 us
    split x0 -> x1, local copies, waits for them, and re-layouts: none -> 17.4 us  [per_device(): jnp.split(lax.all_gather(jnp.concatenate([keys_local, values_local], axis...]
    all_gather x2 -> x1, waiting for transfers between devices: 173 us -> 177 us  [per_device(): lax.all_gather(jnp.concatenate([keys_local, values_local], axis=1), ('row...]
  transfers between devices with their start and end apart: 4 -> 3, of which waited for: 4 -> 3; matrix products, arithmetic and copies ran while one was open for 10% -> 0% of each run, Pallas kernels for 0% -> 0%
where the time goes in v1:
time: 739 us; the launch traced here: 738 us
  waiting for transfers between devices  247 us (33%)
  matrix products  231 us (31%)
  other arithmetic  122 us (17%)
  local copies, waits for them, and re-layouts  121 us (16%)
  between operations  13.3 us (2%)
    all_gather x1, waiting for transfers between devices, per_device(): lax.all_gather(jnp.concatenate([keys_local, values_local], axis=1), ('row...  177 us
    dot_general x32, matrix products, one_block(): jnp.einsum('hqk,khe->hqe', weights.astype(jnp.bfloat16), values, preferre...  145 us
    reduce_sum x32, other arithmetic, one_block(): total = total * factor + jnp.sum(weights, axis=-1)  110 us
    dot_general x32, matrix products, one_block(): jnp.einsum('qhe,khe->hqk', rows, keys, preferred_element_type=jnp.float32)  78.9 us
    while x3, local copies, waits for them, and re-layouts, per_device(): result, unused = lax.scan(step, initial, (kblocks, vblocks))  41.4 us
    all_gather x1, waiting for transfers between devices, per_device(): whole = lax.all_gather(tokens, 'heads', axis=1, tiled=True)  37.4 us
    reduce_scatter x1, waiting for transfers between devices, per_device(): lax.psum_scatter(partial_value.astype(jnp.bfloat16), 'heads', scatter_dim...  32 us
    squeeze x16, local copies, waits for them, and re-layouts, per_device(): result, unused = lax.scan(step, initial, (kblocks, vblocks))  28.4 us
  transfers between devices with their start and end apart: 3, of which 3 were waited for; matrix products, arithmetic and copies ran while one was open for 0% of the time, Pallas kernels for 0%

profile of v1, /device:TPU:0, one launch (start us, length us, event | category | flops | bytes accessed | tf_op | source)
XLA Modules:
  0.0 738.3 jit_solution(8367087247084962209)
XLA Ops:
  7.3 37.4 %all-gather.3.cloned.1.call-done = bf16[1024,1024]{1,0:T(8,128)(2,1)} async-done(((bf16[1024,512]{1,0:T(8,128)(2,1)}), bf16[1024,1024]{1,0:T(8,128)(2,1)}) %all-gather.3.cloned.1.call-update) | async-done | bytes 2097168 | tf_op jit(solution)/shard_map/all_gather | solution.py:29
  56.5 176.8 %all-gather.5.cloned.1.call-done = bf16[16384,1024]{0,1:T(8,128)(2,1)} async-done(((bf16[1024,1024]{0,1:T(8,128)(2,1)}), bf16[16384,1024]{0,1:T(8,128)(2,1)}) %all-gather.5.cloned.1.call-update) | async-done | bytes 33554448 | tf_op jit(solution)/shard_map/all_gather | solution.py:53
  233.3 17.4 %fusion.32 = (bf16[16384,512]{0,1:T(8,128)(2,1)S(1)}, bf16[16384,512]{0,1:T(8,128)(2,1)}) fusion(bf16[16384,1024]{0,1:T(8,128)(2,1)} %all-gather.5.cloned.1.call-done), kind=kLoop, calls=%fused_computation.45 | loop fusion | bytes 67108864 | tf_op jit(solution)/shard_map/split | solution.py:52
  250.7 15.6 %copy.16 = bf16[64,8,16,1024]{3,2,1,0:T(8,128)(2,1)S(1)} copy(bf16[64,8,16,1024]{3,1,2,0:T(8,128)(2,1)} %bitcast.87) | data formatting | bytes 33554432
  266.4 20.6 %copy.11 = bf16[16,1024,8,64]{1,3,2,0:T(8,128)(2,1)} copy(bf16[16,1024,8,64]{1,0,3,2:T(8,128)(2,1)S(1)} %bitcast.84) | data formatting | bytes 33554432 | tf_op jit(solution)/shard_map/while | solution.py:70
  287.0 10.4 %copy.17 = bf16[64,8,16,1024]{3,2,1,0:T(8,128)(2,1)S(1)} copy(bf16[64,8,16,1024]{3,1,2,0:T(8,128)(2,1)S(1)} %bitcast.86) | data formatting | bytes 33554432
  297.4 20.6 %copy.12 = bf16[16,1024,8,64]{1,3,2,0:T(8,128)(2,1)} copy(bf16[16,1024,8,64]{1,0,3,2:T(8,128)(2,1)S(1)} %bitcast.85) | data formatting | bytes 33554432 | tf_op jit(solution)/shard_map/while | solution.py:70
  319.6 371.2 %while.30 = (s32[]{:T(128)}, f32[2,8,512]{2,1,0:T(8,128)S(1)}, f32[2,8,512]{2,1,0:T(8,128)S(1)}, f32[2,8,512,64]{2,3,1,0:T(8,128)}, bf16[16,1024,8,64]{1,3,2,0:T...) while((s32[]{:T(128)}, f32[2,8,512]{2,1,0:T(8,128)S(1)}, ...), condition=%wide.region_7.8_spmd, body=%wide.region_2.7_spmd.sunk | while | flops 1107836928 | bytes 86753680 | solution.py:70
  321.4 21.4 %while.31 = (s32[]{:T(128)}, f32[2,8,512]{2,1,0:T(8,128)S(1)}, f32[2,8,512]{2,1,0:T(8,128)S(1)}, f32[2,8,512,64]{2,3,1,0:T(8,128)}, bf16[2,512,8,64]{1,3,2,0:T(8...) while((s32[]{:T(128)}, f32[2,8,512]{2,1,0:T(8,128)S(1)}, ...), condition=%wide.region_6.6_spmd.clone, body=%wide.region_3.5_spmd.clone.sunk | while | flops 1107836928 | bytes 82559200 | solution.py:25
  324.0 4.5 fusion.52
  334.7 4.5 fusion.52
  344.6 21.4 %while.31 = (s32[]{:T(128)}, f32[2,8,512]{2,1,0:T(8,128)S(1)}, f32[2,8,512]{2,1,0:T(8,128)S(1)}, f32[2,8,512,64]{2,3,1,0:T(8,128)}, bf16[2,512,8,64]{1,3,2,0:T(8...) while((s32[]{:T(128)}, f32[2,8,512]{2,1,0:T(8,128)S(1)}, ...), condition=%wide.region_6.6_spmd.clone, body=%wide.region_3.5_spmd.clone.sunk | while | flops 1107836928 | bytes 82559200 | solution.py:25
  347.2 4.5 fusion.52
  357.9 4.5 fusion.52
  367.8 21.4 %while.31 = (s32[]{:T(128)}, f32[2,8,512]{2,1,0:T(8,128)S(1)}, f32[2,8,512]{2,1,0:T(8,128)S(1)}, f32[2,8,512,64]{2,3,1,0:T(8,128)}, bf16[2,512,8,64]{1,3,2,0:T(8...) while((s32[]{:T(128)}, f32[2,8,512]{2,1,0:T(8,128)S(1)}, ...), condition=%wide.region_6.6_spmd.clone, body=%wide.region_3.5_spmd.clone.sunk | while | flops 1107836928 | bytes 82559200 | solution.py:25
  370.4 4.5 fusion.52
  391.0 21.4 %while.31 = (s32[]{:T(128)}, f32[2,8,512]{2,1,0:T(8,128)S(1)}, f32[2,8,512]{2,1,0:T(8,128)S(1)}, f32[2,8,512,64]{2,3,1,0:T(8,128)}, bf16[2,512,8,64]{1,3,2,0:T(8...) while((s32[]{:T(128)}, f32[2,8,512]{2,1,0:T(8,128)S(1)}, ...), condition=%wide.region_6.6_spmd.clone, body=%wide.region_3.5_spmd.clone.sunk | while | flops 1107836928 | bytes 82559200 | solution.py:25
  393.6 4.5 fusion.52
  414.2 21.4 %while.31 = (s32[]{:T(128)}, f32[2,8,512]{2,1,0:T(8,128)S(1)}, f32[2,8,512]{2,1,0:T(8,128)S(1)}, f32[2,8,512,64]{2,3,1,0:T(8,128)}, bf16[2,512,8,64]{1,3,2,0:T(8...) while((s32[]{:T(128)}, f32[2,8,512]{2,1,0:T(8,128)S(1)}, ...), condition=%wide.region_6.6_spmd.clone, body=%wide.region_3.5_spmd.clone.sunk | while | flops 1107836928 | bytes 82559200 | solution.py:25
  416.8 4.5 fusion.52
  437.4 21.4 %while.31 = (s32[]{:T(128)}, f32[2,8,512]{2,1,0:T(8,128)S(1)}, f32[2,8,512]{2,1,0:T(8,128)S(1)}, f32[2,8,512,64]{2,3,1,0:T(8,128)}, bf16[2,512,8,64]{1,3,2,0:T(8...) while((s32[]{:T(128)}, f32[2,8,512]{2,1,0:T(8,128)S(1)}, ...), condition=%wide.region_6.6_spmd.clone, body=%wide.region_3.5_spmd.clone.sunk | while | flops 1107836928 | bytes 82559200 | solution.py:25
  440.0 4.5 fusion.52
  460.6 21.4 %while.31 = (s32[]{:T(128)}, f32[2,8,512]{2,1,0:T(8,128)S(1)}, f32[2,8,512]{2,1,0:T(8,128)S(1)}, f32[2,8,512,64]{2,3,1,0:T(8,128)}, bf16[2,512,8,64]{1,3,2,0:T(8...) while((s32[]{:T(128)}, f32[2,8,512]{2,1,0:T(8,128)S(1)}, ...), condition=%wide.region_6.6_spmd.clone, body=%wide.region_3.5_spmd.clone.sunk | while | flops 1107836928 | bytes 82559200 | solution.py:25
  463.2 4.5 fusion.52
  483.8 21.4 %while.31 = (s32[]{:T(128)}, f32[2,8,512]{2,1,0:T(8,128)S(1)}, f32[2,8,512]{2,1,0:T(8,128)S(1)}, f32[2,8,512,64]{2,3,1,0:T(8,128)}, bf16[2,512,8,64]{1,3,2,0:T(8...) while((s32[]{:T(128)}, f32[2,8,512]{2,1,0:T(8,128)S(1)}, ...), condition=%wide.region_6.6_spmd.clone, body=%wide.region_3.5_spmd.clone.sunk | while | flops 1107836928 | bytes 82559200 | solution.py:25
  486.4 4.5 fusion.52
  507.0 21.4 %while.31 = (s32[]{:T(128)}, f32[2,8,512]{2,1,0:T(8,128)S(1)}, f32[2,8,512]{2,1,0:T(8,128)S(1)}, f32[2,8,512,64]{2,3,1,0:T(8,128)}, bf16[2,512,8,64]{1,3,2,0:T(8...) while((s32[]{:T(128)}, f32[2,8,512]{2,1,0:T(8,128)S(1)}, ...), condition=%wide.region_6.6_spmd.clone, body=%wide.region_3.5_spmd.clone.sunk | while | flops 1107836928 | bytes 82559200 | solution.py:25
  509.6 4.5 fusion.52
  520.3 4.5 fusion.52
  530.2 21.4 %while.31 = (s32[]{:T(128)}, f32[2,8,512]{2,1,0:T(8,128)S(1)}, f32[2,8,512]{2,1,0:T(8,128)S(1)}, f32[2,8,512,64]{2,3,1,0:T(8,128)}, bf16[2,512,8,64]{1,3,2,0:T(8...) while((s32[]{:T(128)}, f32[2,8,512]{2,1,0:T(8,128)S(1)}, ...), condition=%wide.region_6.6_spmd.clone, body=%wide.region_3.5_spmd.clone.sunk | while | flops 1107836928 | bytes 82559200 | solution.py:25
  532.8 4.5 fusion.52
  543.5 4.5 fusion.52
  553.4 21.4 %while.31 = (s32[]{:T(128)}, f32[2,8,512]{2,1,0:T(8,128)S(1)}, f32[2,8,512]{2,1,0:T(8,128)S(1)}, f32[2,8,512,64]{2,3,1,0:T(8,128)}, bf16[2,512,8,64]{1,3,2,0:T(8...) while((s32[]{:T(128)}, f32[2,8,512]{2,1,0:T(8,128)S(1)}, ...), condition=%wide.region_6.6_spmd.clone, body=%wide.region_3.5_spmd.clone.sunk | while | flops 1107836928 | bytes 82559200 | solution.py:25
  556.0 4.5 fusion.52
  566.7 4.5 fusion.52
  576.6 21.4 %while.31 = (s32[]{:T(128)}, f32[2,8,512]{2,1,0:T(8,128)S(1)}, f32[2,8,512]{2,1,0:T(8,128)S(1)}, f32[2,8,512,64]{2,3,1,0:T(8,128)}, bf16[2,512,8,64]{1,3,2,0:T(8...) while((s32[]{:T(128)}, f32[2,8,512]{2,1,0:T(8,128)S(1)}, ...), condition=%wide.region_6.6_spmd.clone, body=%wide.region_3.5_spmd.clone.sunk | while | flops 1107836928 | bytes 82559200 | solution.py:25
  579.2 4.5 fusion.52
  589.9 4.5 fusion.52
  599.8 21.4 %while.31 = (s32[]{:T(128)}, f32[2,8,512]{2,1,0:T(8,128)S(1)}, f32[2,8,512]{2,1,0:T(8,128)S(1)}, f32[2,8,512,64]{2,3,1,0:T(8,128)}, bf16[2,512,8,64]{1,3,2,0:T(8...) while((s32[]{:T(128)}, f32[2,8,512]{2,1,0:T(8,128)S(1)}, ...), condition=%wide.region_6.6_spmd.clone, body=%wide.region_3.5_spmd.clone.sunk | while | flops 1107836928 | bytes 82559200 | solution.py:25
  602.5 4.5 fusion.52
  613.1 4.5 fusion.52
  623.0 21.4 %while.31 = (s32[]{:T(128)}, f32[2,8,512]{2,1,0:T(8,128)S(1)}, f32[2,8,512]{2,1,0:T(8,128)S(1)}, f32[2,8,512,64]{2,3,1,0:T(8,128)}, bf16[2,512,8,64]{1,3,2,0:T(8...) while((s32[]{:T(128)}, f32[2,8,512]{2,1,0:T(8,128)S(1)}, ...), condition=%wide.region_6.6_spmd.clone, body=%wide.region_3.5_spmd.clone.sunk | while | flops 1107836928 | bytes 82559200 | solution.py:25
  625.7 4.5 fusion.52
  646.2 21.4 %while.31 = (s32[]{:T(128)}, f32[2,8,512]{2,1,0:T(8,128)S(1)}, f32[2,8,512]{2,1,0:T(8,128)S(1)}, f32[2,8,512,64]{2,3,1,0:T(8,128)}, bf16[2,512,8,64]{1,3,2,0:T(8...) while((s32[]{:T(128)}, f32[2,8,512]{2,1,0:T(8,128)S(1)}, ...), condition=%wide.region_6.6_spmd.clone, body=%wide.region_3.5_spmd.clone.sunk | while | flops 1107836928 | bytes 82559200 | solution.py:25
  648.9 4.5 fusion.52
  669.4 21.4 %while.31 = (s32[]{:T(128)}, f32[2,8,512]{2,1,0:T(8,128)S(1)}, f32[2,8,512]{2,1,0:T(8,128)S(1)}, f32[2,8,512,64]{2,3,1,0:T(8,128)}, bf16[2,512,8,64]{1,3,2,0:T(8...) while((s32[]{:T(128)}, f32[2,8,512]{2,1,0:T(8,128)S(1)}, ...), condition=%wide.region_6.6_spmd.clone, body=%wide.region_3.5_spmd.clone.sunk | while | flops 1107836928 | bytes 82559200 | solution.py:25
  672.1 4.5 fusion.52
  696.9 32.0 %reduce-scatter.2.cloned.1.call-done = bf16[1024,512]{1,0:T(8,128)(2,1)} async-done(((bf16[1024,1024]{1,0:T(8,128)(2,1)}), bf16[1024,512]{1,0:T(8,128)(2,1)}) %reduce-scatter.2.cloned.1.call-update) | async-done | bytes 1048592 | tf_op jit(solution)/shard_map/reduce_scatter | solution.py:79
  (476 shorter events, 285.7 us)
Async XLA Ops:
  6.5 42.6 %copy-start = (bf16[3,1024,512]{2,1,0:T(8,128)(2,1)S(1)}, bf16[3,1024,512]{2,1,0:T(8,128)(2,1)}, u32[]{:S(2)}) copy-start(bf16[3,1024,512]{2,1,0:T(8,128)(2,1)} %param.11) | copy-start | bytes 9437188
  6.5 42.6 %copy-start.9 = (f32[1024]{0:T(1024)S(1)}, f32[1024]{0:T(1024)}, u32[]{:S(2)}) copy-start(f32[1024]{0:T(1024)} %param.10) | copy-start | bytes 12292
  6.5 38.2 %all-gather.3.cloned.1.call-start = ((), (), s32[]{:S(2)}) async-start(), calls=%async_computation.1 | async-start | bytes 3145728 | tf_op jit(solution)/shard_map/all_gather | solution.py:29
  7.3 226.0 %all-gather.5.cloned.1.call-start = ((), (), s32[]{:S(2)}) async-start(), calls=%async_computation.2 | async-start | bytes 35651584 | tf_op jit(solution)/shard_map/all_gather | solution.py:53
  44.7 4.4 copy-start.6
  55.3 673.6 %reduce-scatter.2.cloned.1.call-start = ((), (), s32[]{:S(2)}) async-start(), calls=%async_computation.3 | async-start | bytes 3145728 | tf_op jit(solution)/shard_map/reduce_scatter | solution.py:79
  328.6 3.5 copy-start.3
  328.6 3.5 copy-start.5
  339.3 3.5 copy-start.3
  339.3 3.5 copy-start.5
  351.8 3.5 copy-start.5
  362.5 3.5 copy-start.3
  362.5 3.5 copy-start.5
  375.0 3.5 copy-start.3
  375.0 3.5 copy-start.5
  385.7 3.5 copy-start.3
  385.7 3.5 copy-start.5
  398.2 3.5 copy-start.3
  398.2 3.5 copy-start.5
  408.9 3.5 copy-start.3
  408.9 3.5 copy-start.5
  421.4 3.5 copy-start.3
  421.4 3.5 copy-start.5
  432.1 3.5 copy-start.5
  444.6 3.5 copy-start.5
  455.3 3.5 copy-start.5
  467.8 3.5 copy-start.5
  478.5 3.5 copy-start.5
  491.0 3.5 copy-start.5
  501.7 3.5 copy-start.5
  514.2 3.5 copy-start.5
  524.9 3.5 copy-start.5
  537.4 3.5 copy-start.5
  548.1 3.5 copy-start.5
  560.6 3.5 copy-start.5
  571.3 3.5 copy-start.5
  583.8 3.5 copy-start.5
  594.5 3.5 copy-start.5
  607.0 3.5 copy-start.5
  617.7 3.5 copy-start.5
  630.2 3.5 copy-start.5
  640.9 3.5 copy-start.5
  653.4 3.5 copy-start.5
  664.1 3.5 copy-start.5
  676.6 3.5 copy-start.5
  687.3 3.5 copy-start.5
  694.2 34.7 %copy-start.7 = (f32[512]{0:T(512)S(1)}, f32[512]{0:T(512)}, u32[]{:S(2)}) copy-start(f32[512]{0:T(512)} %param.13) | copy-start | bytes 6148
  694.2 37.5 %copy-start.1 = (bf16[3,1024,512]{2,1,0:T(8,128)(2,1)S(1)}, bf16[3,1024,512]{2,1,0:T(8,128)(2,1)}, u32[]{:S(2)}) copy-start(bf16[3,1024,512]{2,1,0:T(8,128)(2,1)} %param.11) | copy-start | bytes 9437188
  (89 other events, 246.9 us)
Sparse Core Ops, SparseCore 0:
  8.9 35.8 all-gather.2
  55.4 177.8 all-gather.4
  697.0 31.8 reduce-scatter.1
